TPU v7x, 32 devices: a whole 2x2x4 slice. The times are simulated.
32 devices in a mesh: lat: 8 (over y, x, core), lon: 4 (over z).
Axes of the slice: x: 2, y: 2, z: 4, core: 2. Of those that a mesh axis runs over, the one named last changes fastest.
Arguments:
- coeffs_old: float32 [640, 2, 3, 50, 640], P(('lat', 'lon')), may hold values from -0.16 to 0.16
- noise: bfloat16 [640, 2, 3, 50, 640], P(('lat', 'lon')), may hold values from -6 to 6
- legendre: float32 [640, 640, 640], P(('lat', 'lon')), may hold values from -0.25 to 0.25
- decay: float32 [3], replicated, may hold values from 0.3 to 0.97
- amplitude: float32 [3, 640], replicated, may hold values from 0.005 to 0.05
- wavenumber_of_slot: int32 [640], replicated, may hold values from 0 to 639, as said below
- lat_order: int32 [640], replicated, may hold values from 0 to 639, each once
Outputs:
- coeffs_new: float32 [640, 2, 3, 50, 640], P(('lat', 'lon'))
- pattern: float32 [640, 50, 1280], P(('lat', 'lon'))
Inputs may be any that keep to these rules, and one draw needn't show every extreme that they name: `wavenumber_of_slot`: every wavenumber fills exactly one slot; the sums of the wavenumbers of one device's 20 slots differ between devices by less than 32. `lat_order`: every latitude stands in exactly one row.
All inputs are finite; a program needn't handle non-finite values.
Results may differ from a plain program's by a relative error of at most 0.0003.
Values sent between devices are 32-bit elements; how exact they have to be, the bound alone decides.
A program may use at most 192 MiB of HBM per device.

v0:
```python
import jax
import jax.numpy as jnp
from jax import lax
from jax.sharding import PartitionSpec as P

LON = 1280
TWO_PI = 6.283185307179586


def evolve(coeffs_old, noise, decay, amplitude, waves):
    width = coeffs_old.shape[4]
    offsets = lax.broadcasted_iota(jnp.int32, (waves.shape[0], width), 1)
    live = waves[:, None] + offsets < width
    padded = jnp.concatenate([amplitude, jnp.zeros_like(amplitude)], axis=1)
    spread = jax.vmap(lambda wave: lax.dynamic_slice_in_dim(padded, wave, width, 1))(waves)
    factor = jnp.sqrt(1.0 - decay * decay)
    fresh = decay[None, None, :, None, None] * coeffs_old + (spread * factor[None, :, None])[
        :, None, :, None, :
    ] * noise.astype(jnp.float32)
    return jnp.where(live[:, None, None, None, :], fresh, jnp.zeros_like(fresh))


def synthesis_table(waves, length):
    column = lax.broadcasted_iota(jnp.int32, (waves.shape[0], length), 1)
    phase = waves[:, None] * column % length
    angle = phase.astype(jnp.float32) * (TWO_PI / length)
    weight = jnp.where(waves == 0, 1.0, 2.0).astype(jnp.float32)[:, None]
    return jnp.stack([weight * jnp.cos(angle), -weight * jnp.sin(angle)], axis=1)


def synthesize(values, table):
    return jnp.einsum("sreq,srl->qel", values, table, precision=lax.Precision.HIGHEST)


def local(coeffs_old, noise, legendre, decay, amplitude, wavenumber_of_slot, lat_order):
    lat_count = lax.axis_size("lat")
    lon_count = lax.axis_size("lon")
    lat_index = lax.axis_index("lat")
    lon_index = lax.axis_index("lon")
    slots = coeffs_old.shape[0]
    mine = lax.dynamic_slice_in_dim(
        wavenumber_of_slot, (lat_index * lon_count + lon_index) * slots, slots
    )
    coeffs_new = evolve(coeffs_old, noise, decay, amplitude, mine)
    field = jnp.einsum("srkej,slj->srel", coeffs_new, legendre, precision=lax.Precision.HIGHEST)
    field = jnp.take(field, lat_order, axis=3)
    ordered = wavenumber_of_slot.reshape(lat_count, lon_count, slots).transpose(1, 0, 2).reshape(-1)
    full_table = synthesis_table(ordered, LON)
    pattern = synthesize(
        lax.all_to_all(
            lax.all_to_all(field, "lat", split_axis=3, concat_axis=0, tiled=True),
            "lon",
            split_axis=3,
            concat_axis=0,
            tiled=True,
        ),
        full_table,
    )
    return (coeffs_new, pattern)


def solution(mesh):
    in_specs = (
        P(("lat", "lon"), None, None, None, None),
        P(("lat", "lon"), None, None, None, None),
        P(("lat", "lon"), None, None),
        P(),
        P(),
        P(),
        P(),
    )
    out_specs = (P(("lat", "lon"), None, None, None, None), P(("lat", "lon"), None, None))
    return jax.shard_map(local, mesh=mesh, in_specs=in_specs, out_specs=out_specs, check_vma=False)
```

profile of v0, /device:TPU:0, one launch (start us, length us, event | category | flops | bytes accessed | tf_op | source)
XLA Modules:
  0.0 590.6 jit_solution(11389839738425668350)
XLA Ops:
  2.0 0.8 fusion.12
  3.5 26.4 %while.1 = (s32[]{:T(128)}, f32[3,1280]{1,0:T(4,128)S(1)}, s32[20,2]{0,1:T(2,128)S(1)}, f32[20,3,640]{2,1,0:T(4,128)S(1)}, s32[]{:T(128)}) while((s32[]{:T(128)}, f32[3,1280]{1,0:T(4,128)S(1)}, s32[20,2]{0,1:T(2,128)S(1)}, f32[20,3,640]{2,1,0:T(4,128)S(1)}, s32[]{:T(128)}) %tuple.24), condition=%wide.while_cond, body=%wide.while_body.sunk | while | flops 2 | bytes 20585 | solution.py:15
  4.1 0.7 bitcast_dynamic-update-slice_fusion.2
  5.4 0.7 bitcast_dynamic-update-slice_fusion.2
  6.7 0.7 bitcast_dynamic-update-slice_fusion.2
  8.1 0.7 bitcast_dynamic-update-slice_fusion.2
  9.4 0.7 bitcast_dynamic-update-slice_fusion.2
  10.7 0.7 bitcast_dynamic-update-slice_fusion.2
  12.0 0.7 bitcast_dynamic-update-slice_fusion.2
  13.3 0.7 bitcast_dynamic-update-slice_fusion.2
  14.7 0.7 bitcast_dynamic-update-slice_fusion.2
  16.0 0.7 bitcast_dynamic-update-slice_fusion.2
  17.3 0.7 bitcast_dynamic-update-slice_fusion.2
  18.6 0.7 bitcast_dynamic-update-slice_fusion.2
  30.8 32.2 %fusion.15 = (f32[20,2,50,640]{3,1,2,0:T(2,128)}, f32[20,2,3,50,640]{4,1,3,2,0:T(2,128)}) fusion(bf16[20,2,3,50,640]{4,1,3,2,0:T(2,128)(2,1)} %param.8, f32[20,3,640]{2,1,0:T(4,128)S(1)} %broadcast_multiply_fusion, f32[20,2,3,50,640]{4,1,3,2,0:T(2,128)} %param.7, f32[3]{0:T(128)} %param.10, pred[20,640]{1,0:T(8,128)(4,1)S(1)} %add_compare_fusion), kind=kLoop, calls=%fused_computation.33 | loop fusion | flops 21760000 | bytes 43686412 | tf_op jit(solution)/shard_map/srkej,slj->srel/reduce_sum | solution.py:45
  63.0 36.1 %fusion = f32[20,2,50,640]{3,2,1,0:T(8,128)} fusion(f32[20,640,640]{2,1,0:T(8,128)} %param.9, f32[20,2,50,640]{3,1,2,0:T(2,128)} %get-tuple-element.18), kind=kOutput, calls=%fused_computation.3 | convolution fusion | flops 9830400000 | bytes 43008000 | tf_op jit(solution)/shard_map/srkej,slj->srel/dot_general | solution.py:45
  99.1 15.9 %copy.33 = f32[20,2,50,640]{2,1,3,0:T(2,128)} copy(f32[20,2,50,640]{3,2,1,0:T(8,128)} %fusion) | data formatting | bytes 10240000 | tf_op jit(solution)/shard_map/srkej,slj->srel/dot_general | solution.py:45
  115.0 38.6 %gather_fusion = f32[640,20,2,50]{3,2,1,0:T(2,128)} fusion(f32[20,2,50,640]{2,1,3,0:T(2,128)} %copy.33, s32[1024]{0:T(1024)S(1)} %pad_clamp_fusion), kind=kCustom, calls=%fused_computation | custom fusion | bytes 10242560 | tf_op jit(solution)/shard_map/jit(_take)/gather | solution.py:46
  153.6 10.2 %fusion.16 = f32[640,20,2,50]{3,2,1,0:T(2,128)} fusion(f32[640,20,2,50]{3,2,1,0:T(2,128)} %gather_fusion, pred[640]{0:T(1024)(128)(4,1)S(1)} %compare_and_fusion), kind=kLoop, calls=%fused_computation.34 | loop fusion | flops 1280000 | bytes 10240640
  163.8 27.8 %reshape.218 = f32[8,1,160000]{2,1,0:T(1,128)} reshape(f32[640,20,2,50]{3,2,1,0:T(2,128)} %fusion.16) | data formatting | bytes 10240000
  191.5 64.3 %all_to_all.36 = f32[8,1,160000]{2,1,0:T(1,128)} all-to-all(f32[8,1,160000]{2,1,0:T(1,128)} %reshape.218), channel_id=1, replica_groups=mesh['lat'=8,'lon'=4] {'lat'}, dimensions={0} | all-to-all | bytes 10240000 | tf_op jit(solution)/shard_map/all_to_all | solution.py:51
  256.3 17.0 %reduce = f32[8,160000]{1,0:T(8,128)} reduce(f32[8,1,160000]{2,1,0:T(1,128)} %all_to_all.36, f32[]{:T(128)} %broadcast.203), dimensions={1}, to_apply=%all_to_all.26.reduce_sub_computation | reduce | bytes 10240004 | tf_op jit(solution)/shard_map/all_to_all | solution.py:51
  273.3 33.3 %reshape.219 = f32[640,20,2,50]{3,2,1,0:T(2,128)} reshape(f32[8,160000]{1,0:T(8,128)} %reduce) | data formatting | bytes 10240000
  306.6 17.1 %copy.42 = f32[20,2,50,8,80]{4,3,1,2,0:T(8,128)} copy(f32[20,2,50,8,80]{2,1,0,4,3:T(2,128)} %bitcast.41) | data formatting | bytes 10240000 | tf_op jit(solution)/shard_map/all_to_all | solution.py:51
  323.7 13.0 %copy.35 = f32[8,20,2,50,80]{4,2,3,1,0:T(2,128)} copy(f32[8,20,2,50,80]{4,0,2,3,1:T(8,128)} %bitcast.43) | data formatting | bytes 10240000 | tf_op jit(solution)/shard_map/all_to_all | solution.py:51
  336.7 18.0 %copy.36 = f32[160,2,50,80]{0,1,2,3:T(2,128)} copy(f32[160,2,50,80]{3,1,2,0:T(2,128)} %bitcast.42) | data formatting | bytes 10240000 | tf_op jit(solution)/shard_map/all_to_all | solution.py:51
  354.7 5.7 all-to-all-start.1
  360.7 15.2 %cosine_multiply_fusion = (f32[640,1,1280]{2,0,1:T(8,128)S(1)}, f32[640,1,1280]{2,0,1:T(8,128)}) fusion(s32[640]{0:T(1024)S(1)} %reshape.185, f32[640]{0:T(1024)S(1)} %get-tuple-element.24, f32[640]{0:T(1024)S(1)} %get-tuple-element.25), kind=kLoop, calls=%fused_computation.17 | loop fusion | flops 9011200 | bytes 6561280 | tf_op jit(solution)/shard_map/mul | solution.py:28
  375.9 164.0 %all-to-all-done.1 = f32[160,2,50,80]{0,1,2,3:T(2,128)} async-done(((f32[160,2,50,80]{0,1,2,3:T(2,128)}), f32[160,2,50,80]{0,1,2,3:T(2,128)}, u32[]{:S(2)}, u32[]{:S(2)}) %all-to-all-start.1) | async-done | bytes 5120032 | tf_op jit(solution)/shard_map/all_to_all | solution.py:50
  539.9 11.8 %copy.44 = f32[4,160,2,50,20]{1,0,3,2,4:T(4,128)} copy(f32[4,160,2,50,20]{1,2,3,4,0:T(2,128)} %bitcast.11) | data formatting | bytes 10240000 | tf_op jit(solution)/shard_map/all_to_all | solution.py:50
  551.7 9.5 %reshape.217 = f32[640,2,50,20]{0,2,1,3:T(8,128)} reshape(f32[4,160,2,50,20]{1,0,3,2,4:T(4,128)} %copy.44) | data formatting | bytes 10240000 | tf_op jit(solution)/shard_map/all_to_all | solution.py:50
  561.3 29.1 %fusion.6 = f32[20,50,1280]{2,1,0:T(8,128)} fusion(f32[640,2,50,20]{0,2,1,3:T(8,128)} %reshape.217, f32[640,1,1280]{2,0,1:T(8,128)} %get-tuple-element.23, f32[640,1,1280]{2,0,1:T(8,128)S(1)} %get-tuple-element.22), kind=kOutput, calls=%fused_computation.13 | convolution fusion | flops 19662438400 | bytes 16793600 | tf_op jit(solution)/shard_map/sreq,srl->qel/dot_general | solution.py:32
  (64 shorter events, 21.3 us)
Async XLA Ops:
  354.7 5.8 copy-start
  354.7 185.2 %all-to-all-start.1 = ((f32[160,2,50,80]{0,1,2,3:T(2,128)}), f32[160,2,50,80]{0,1,2,3:T(2,128)}, u32[]{:S(2)}, u32[]{:S(2)}) async-start(f32[160,2,50,80]{0,1,2,3:T(2,128)} %copy.36), calls=%async_computation.1 | async-start | bytes 16384000 | tf_op jit(solution)/shard_map/all_to_all | solution.py:50
where the time goes:
time: 601 us; the launch traced here: 591 us
  local copies, waits for them, and re-layouts  213 us (35%)
  waiting for transfers between devices  164 us (27%)
  other arithmetic  77.6 us (13%)
  matrix products  65.2 us (11%)
  blocking collectives  64.3 us (11%)
    all_to_all x1, waiting for transfers between devices, local(): lax.all_to_all(lax.all_to_all(field, 'lat', split_axis=3, concat_axis=0,...  164 us
    all_to_all x1, blocking collectives, local(): lax.all_to_all(field, 'lat', split_axis=3, concat_axis=0, tiled=True)  64.3 us
    unnamed x4, local copies, waits for them, and re-layouts  61.1 us
    all_to_all x4, local copies, waits for them, and re-layouts, local(): lax.all_to_all(field, 'lat', split_axis=3, concat_axis=0, tiled=True)  48.6 us
    gather x1, local copies, waits for them, and re-layouts, local(): field = jnp.take(field, lat_order, axis=3)  38.6 us
    dot_general x1, matrix products, local(): jnp.einsum('srkej,slj->srel', coeffs_new, legendre, precision=lax.Precisi...  36.1 us
    reduce_sum x1, other arithmetic, local(): jnp.einsum('srkej,slj->srel', coeffs_new, legendre, precision=lax.Precisi...  32.2 us
    dot_general x1, matrix products, synthesize(): jnp.einsum('sreq,srl->qel', values, table, precision=lax.Precision.HIGHEST)  29.1 us
  transfers between devices with their start and end apart: 1, of which 1 were waited for; matrix products, arithmetic and copies ran while one was open for 3% of the time, Pallas kernels for 0%

commit v1 on v0

--- a/solution.py
+++ b/solution.py
@@ -5,6 +5,18 @@
 
 LON = 1280
 TWO_PI = 6.283185307179586
+
+
+def exchange_directly(shard, axis, split, join):
+    ways, here = (lax.axis_size(axis), lax.axis_index(axis))
+    width = shard.shape[split] // ways
+    turned = jnp.roll(shard, -here * width, axis=split)
+    got = [lax.slice_in_dim(turned, 0, width, axis=split)]
+    for far in range(1, ways):
+        sent = lax.slice_in_dim(turned, far * width, (far + 1) * width, axis=split)
+        got.append(lax.ppermute(sent, axis, [(d, (d + far) % ways) for d in range(ways)]))
+    line = jnp.concatenate(got[::-1], axis=join)
+    return jnp.roll(line, (here + 1) * got[0].shape[join], axis=join)
 
 
 def evolve(coeffs_old, noise, decay, amplitude, waves):
@@ -48,11 +60,7 @@
     full_table = synthesis_table(ordered, LON)
     pattern = synthesize(
         lax.all_to_all(
-            lax.all_to_all(field, "lat", split_axis=3, concat_axis=0, tiled=True),
-            "lon",
-            split_axis=3,
-            concat_axis=0,
-            tiled=True,
+            exchange_directly(field, "lat", 3, 0), "lon", split_axis=3, concat_axis=0, tiled=True
         ),
         full_table,
     )

time: 601 us -> 580 us (0.965)
  waiting for transfers between devices: 164 us -> 250 us
  blocking collectives: 64.3 us -> 0 us
  local copies, waits for them, and re-layouts: 213 us -> 165 us
  starting transfers between devices: 5.75 us -> 12.4 us
    ppermute x0 -> x7, waiting for transfers between devices: none -> 88.3 us  [exchange_directly(): lax.ppermute(sent, axis, [(d, (d + far) % ways) for d in range(ways)])]
    all_to_all x1 -> x0, blocking collectives: 64.3 us -> none  [local(): lax.all_to_all(field, 'lat', split_axis=3, concat_axis=0, tiled=True)]
    unnamed x4 -> x17, local copies, waits for them, and re-layouts: 61.1 us -> 8.09 us
    all_to_all x6 -> x2, local copies, waits for them, and re-layouts: 69.9 us -> 21.3 us  [local(): lax.all_to_all(exchange_directly(field, 'lat', 3, 0), 'lon', split_axis=3...]
    dynamic_slice x0 -> x2, local copies, waits for them, and re-layouts: none -> 21.5 us  [exchange_directly(): return jnp.roll(line, (here + 1) * got[0].shape[join], axis=join)]
    select_n x0 -> x1, local copies, waits for them, and re-layouts: none -> 18.7 us  [local(): field = jnp.take(field, lat_order, axis=3)]
    all_to_all x1 -> x0, other arithmetic: 17 us -> none  [local(): lax.all_to_all(field, 'lat', split_axis=3, concat_axis=0, tiled=True)]
    concatenate x0 -> x1, other arithmetic: none -> 15.3 us  [exchange_directly(): turned = jnp.roll(shard, -here * width, axis=split)]
  transfers between devices with their start and end apart: 1 -> 8, of which waited for: 1 -> 4; matrix products, arithmetic and copies ran while one was open for 3% -> 3% of each run, Pallas kernels for 0% -> 0%
where the time goes in v1:
time: 580 us; the launch traced here: 570 us
  waiting for transfers between devices  250 us (43%)
  local copies, waits for them, and re-layouts  165 us (28%)
  other arithmetic  75.9 us (13%)
  matrix products  65.1 us (11%)
  starting transfers between devices  12.4 us (2%)
    all_to_all x1, waiting for transfers between devices, local(): lax.all_to_all(exchange_directly(field, 'lat', 3, 0), 'lon', split_axis=3...  161 us
    ppermute x7, waiting for transfers between devices, exchange_directly(): lax.ppermute(sent, axis, [(d, (d + far) % ways) for d in range(ways)])  88.3 us
    gather x1, local copies, waits for them, and re-layouts, local(): field = jnp.take(field, lat_order, axis=3)  38.6 us
    dot_general x1, matrix products, local(): jnp.einsum('srkej,slj->srel', coeffs_new, legendre, precision=lax.Precisi...  36.1 us
    reduce_sum x1, other arithmetic, local(): jnp.einsum('srkej,slj->srel', coeffs_new, legendre, precision=lax.Precisi...  32.2 us
    dot_general x1, matrix products, synthesize(): jnp.einsum('sreq,srl->qel', values, table, precision=lax.Precision.HIGHEST)  29.1 us
    gather x60, local copies, waits for them, and re-layouts  26.4 us
    dynamic_slice x2, local copies, waits for them, and re-layouts, exchange_directly(): return jnp.roll(line, (here + 1) * got[0].shape[join], axis=join)  21.5 us
  transfers between devices with their start and end apart: 8, of which 4 were waited for; matrix products, arithmetic and copies ran while one was open for 3% of the time, Pallas kernels for 0%

profile of v1, /device:TPU:0, one launch (start us, length us, event | category | flops | bytes accessed | tf_op | source)
XLA Modules:
  0.0 569.5 jit_solution(8634721079028255793)
XLA Ops:
  2.0 0.8 fusion.13
  3.5 26.4 %while.1 = (s32[]{:T(128)}, f32[3,1280]{1,0:T(4,128)S(1)}, s32[20,2]{0,1:T(2,128)S(1)}, f32[20,3,640]{2,1,0:T(4,128)S(1)}, s32[]{:T(128)}) while((s32[]{:T(128)}, f32[3,1280]{1,0:T(4,128)S(1)}, s32[20,2]{0,1:T(2,128)S(1)}, f32[20,3,640]{2,1,0:T(4,128)S(1)}, s32[]{:T(128)}) %tuple.30), condition=%wide.while_cond, body=%wide.while_body.sunk | while | flops 2 | bytes 20585 | solution.py:27
  4.1 0.7 bitcast_dynamic-update-slice_fusion.2
  5.4 0.7 bitcast_dynamic-update-slice_fusion.2
  10.7 0.7 bitcast_dynamic-update-slice_fusion.2
  30.8 32.2 %fusion.16 = (f32[20,2,50,640]{3,1,2,0:T(2,128)}, f32[20,2,3,50,640]{4,1,3,2,0:T(2,128)}) fusion(bf16[20,2,3,50,640]{4,1,3,2,0:T(2,128)(2,1)} %param.8, f32[20,3,640]{2,1,0:T(4,128)S(1)} %broadcast_multiply_fusion, f32[20,2,3,50,640]{4,1,3,2,0:T(2,128)} %param.7, f32[3]{0:T(128)} %param.10, pred[20,640]{1,0:T(8,128)(4,1)S(1)} %add_compare_fusion), kind=kLoop, calls=%fused_computation.53 | loop fusion | flops 21760000 | bytes 43686412 | tf_op jit(solution)/shard_map/srkej,slj->srel/reduce_sum | solution.py:57
  63.0 36.1 %fusion = f32[20,2,50,640]{3,2,1,0:T(8,128)} fusion(f32[20,640,640]{2,1,0:T(8,128)} %param.9, f32[20,2,50,640]{3,1,2,0:T(2,128)} %get-tuple-element.18), kind=kOutput, calls=%fused_computation.3 | convolution fusion | flops 9830400000 | bytes 43008000 | tf_op jit(solution)/shard_map/srkej,slj->srel/dot_general | solution.py:57
  99.1 15.9 %copy.46 = f32[20,2,50,640]{2,1,3,0:T(2,128)} copy(f32[20,2,50,640]{3,2,1,0:T(8,128)} %fusion) | data formatting | bytes 10240000 | tf_op jit(solution)/shard_map/srkej,slj->srel/dot_general | solution.py:57
  115.0 38.6 %gather_fusion = f32[640,20,2,50]{3,2,1,0:T(2,128)} fusion(f32[20,2,50,640]{2,1,3,0:T(2,128)} %copy.46, s32[1024]{0:T(1024)S(1)} %pad_clamp_fusion), kind=kCustom, calls=%fused_computation | custom fusion | bytes 10242560 | tf_op jit(solution)/shard_map/jit(_take)/gather | solution.py:58
  153.6 10.2 %select_bitcast_fusion = f32[20,2,50,640]{2,1,0,3:T(2,128)} fusion(f32[640,20,2,50]{3,2,1,0:T(2,128)} %gather_fusion, pred[640]{0:T(1024)(128)(4,1)S(1)} %compare_and_fusion), kind=kLoop, calls=%fused_computation.6 | loop fusion | flops 1280000 | bytes 10240640 | tf_op jit(solution)/shard_map/jit(_take)/select_n | solution.py:58
  163.8 18.7 %copy.47 = f32[20,2,50,640]{3,1,2,0:T(2,128)} copy(f32[20,2,50,640]{2,1,0,3:T(2,128)} %select_bitcast_fusion) | data formatting | bytes 10240000 | tf_op jit(solution)/shard_map/jit(_take)/select_n | solution.py:58
  182.5 15.3 %fusion.6 = f32[20,2,50,640]{3,1,2,0:T(2,128)} fusion(s32[]{:T(128)S(6)} %select_n.78, f32[20,2,50,640]{3,1,2,0:T(2,128)} %copy.47), kind=kLoop, calls=%fused_computation.14 | loop fusion | flops 1280000 | bytes 10240004 | tf_op jit(solution)/shard_map/jit(_roll_dynamic)/concatenate | solution.py:13
  197.8 12.5 %fusion.17 = (f32[20,2,50,80]{3,1,2,0:T(2,128)}, f32[20,2,50,80]{3,1,2,0:T(2,128)}, f32[20,2,50,80]{3,1,2,0:T(2,128)}, f32[20,2,50,80]{3,1,2,0:T(2,128)}, f32[20...) fusion(f32[20,2,50,640]{3,1,2,0:T(2,128)} %fusion.6), kind=kLoop, calls=%fused_computation.54 | loop fusion | bytes 8960000 | tf_op jit(solution)/shard_map/slice | solution.py:16
  210.3 3.7 collective-permute-start
  214.9 1.5 collective-permute-start.3
  216.6 20.6 %collective-permute-done = f32[20,2,50,80]{3,1,2,0:T(2,128)S(1)} collective-permute-done((f32[20,2,50,80]{3,1,2,0:T(2,128)}, f32[20,2,50,80]{3,1,2,0:T(2,128)S(1)}, u32[]{:S(2)}, u32[]{:S(2)}) %collective-permute-start) | collective-permute-done | bytes 640032 | tf_op jit(solution)/shard_map/ppermute | solution.py:17
  237.4 21.9 %collective-permute-done.1 = f32[20,2,50,80]{3,1,2,0:T(2,128)S(1)} collective-permute-done((f32[20,2,50,80]{3,1,2,0:T(2,128)}, f32[20,2,50,80]{3,1,2,0:T(2,128)S(1)}, u32[]{:S(2)}, u32[]{:S(2)}) %collective-permute-start.1) | collective-permute-done | bytes 640032 | tf_op jit(solution)/shard_map/ppermute | solution.py:17
  259.6 45.7 %collective-permute-done.3 = f32[20,2,50,80]{3,1,2,0:T(2,128)} collective-permute-done((f32[20,2,50,80]{3,1,2,0:T(2,128)}, f32[20,2,50,80]{3,1,2,0:T(2,128)}, u32[]{:S(2)}, u32[]{:S(2)}) %collective-permute-start.3) | collective-permute-done | bytes 640032 | tf_op jit(solution)/shard_map/ppermute | solution.py:17
  305.3 1.4 constant_dynamic-update-slice_fusion.10
  306.7 1.4 constant_dynamic-update-slice_fusion.9
  308.3 1.4 slice_dynamic-update-slice_fusion
  310.1 1.4 constant_dynamic-update-slice_fusion.3
  311.5 1.4 constant_dynamic-update-slice_fusion.2
  313.1 1.4 slice_dynamic-update-slice_fusion.1
  314.5 3.5 constant_dynamic-slice_fusion.1
  318.0 18.0 %copy.49 = f32[160,2,50,80]{0,1,2,3:T(2,128)} copy(f32[160,2,50,80]{3,1,2,0:T(2,128)} %constant_dynamic-slice_fusion.1) | data formatting | bytes 10240000 | tf_op jit(solution)/shard_map/jit(_roll_dynamic)/dynamic_slice | solution.py:19
  336.0 6.1 %all-to-all-start = ((f32[160,2,50,80]{0,1,2,3:T(2,128)}), f32[160,2,50,80]{0,1,2,3:T(2,128)}, u32[]{:S(2)}, u32[]{:S(2)}) async-start(f32[160,2,50,80]{0,1,2,3:T(2,128)} %copy.49), calls=%async_computation | async-start | bytes 16384000 | tf_op jit(solution)/shard_map/all_to_all | solution.py:62
  342.3 15.2 %cosine_multiply_fusion = (f32[640,1,1280]{2,0,1:T(8,128)S(1)}, f32[640,1,1280]{2,0,1:T(8,128)}) fusion(s32[640]{0:T(1024)S(1)} %reshape.185, f32[640]{0:T(1024)S(1)} %get-tuple-element.31, f32[640]{0:T(1024)S(1)} %get-tuple-element.32), kind=kLoop, calls=%fused_computation.20 | loop fusion | flops 9011200 | bytes 6561280 | tf_op jit(solution)/shard_map/mul | solution.py:40
  357.5 161.4 %all-to-all-done = f32[160,2,50,80]{0,1,2,3:T(2,128)} async-done(((f32[160,2,50,80]{0,1,2,3:T(2,128)}), f32[160,2,50,80]{0,1,2,3:T(2,128)}, u32[]{:S(2)}, u32[]{:S(2)}) %all-to-all-start) | async-done | bytes 5120032 | tf_op jit(solution)/shard_map/all_to_all | solution.py:62
  519.0 11.8 %copy.56 = f32[4,160,2,50,20]{1,0,3,2,4:T(4,128)} copy(f32[4,160,2,50,20]{1,2,3,4,0:T(2,128)} %bitcast.8) | data formatting | bytes 10240000 | tf_op jit(solution)/shard_map/all_to_all | solution.py:62
  530.7 9.6 %reshape.217 = f32[640,2,50,20]{0,2,1,3:T(8,128)} reshape(f32[4,160,2,50,20]{1,0,3,2,4:T(4,128)} %copy.56) | data formatting | bytes 10240000 | tf_op jit(solution)/shard_map/all_to_all | solution.py:62
  540.3 29.1 %fusion.7 = f32[20,50,1280]{2,1,0:T(8,128)} fusion(f32[640,2,50,20]{0,2,1,3:T(8,128)} %reshape.217, f32[640,1,1280]{2,0,1:T(8,128)} %get-tuple-element.30, f32[640,1,1280]{2,0,1:T(8,128)S(1)} %get-tuple-element.29), kind=kOutput, calls=%fused_computation.16 | convolution fusion | flops 19662438400 | bytes 16793600 | tf_op jit(solution)/shard_map/sreq,srl->qel/dot_general | solution.py:44
  (91 shorter events, 29.8 us)
Async XLA Ops:
  210.3 27.0 %collective-permute-start = (f32[20,2,50,80]{3,1,2,0:T(2,128)}, f32[20,2,50,80]{3,1,2,0:T(2,128)S(1)}, u32[]{:S(2)}, u32[]{:S(2)}) collective-permute-start(f32[20,2,50,80]{3,1,2,0:T(2,128)} %get-tuple-element.28), channel_id=1, source_target_pairs={{0,28},{4,0},{8,4},{12,8},{16,12},{20,16},{24,20},{28,24},{1,29},{... | collective-permute-start | bytes 1920008 | tf_op jit(solution)/shard_map/ppermute | solution.py:17
  214.0 45.3 %collective-permute-start.1 = (f32[20,2,50,80]{3,1,2,0:T(2,128)}, f32[20,2,50,80]{3,1,2,0:T(2,128)S(1)}, u32[]{:S(2)}, u32[]{:S(2)}) collective-permute-start(f32[20,2,50,80]{3,1,2,0:T(2,128)} %get-tuple-element.27), channel_id=1, source_target_pairs={{0,24},{4,28},{8,0},{12,4},{16,8},{20,12},{24,16},{28,20},{1,25},{... | collective-permute-start | bytes 1920008 | tf_op jit(solution)/shard_map/ppermute | solution.py:17
  214.6 44.8 %collective-permute-start.2 = (f32[20,2,50,80]{3,1,2,0:T(2,128)}, f32[20,2,50,80]{3,1,2,0:T(2,128)S(1)}, u32[]{:S(2)}, u32[]{:S(2)}) collective-permute-start(f32[20,2,50,80]{3,1,2,0:T(2,128)} %get-tuple-element.26), channel_id=1, source_target_pairs={{0,20},{4,24},{8,28},{12,0},{16,4},{20,8},{24,12},{28,16},{1,21},{... | collective-permute-start | bytes 1920008 | tf_op jit(solution)/shard_map/ppermute | solution.py:17
  214.9 90.3 %collective-permute-start.3 = (f32[20,2,50,80]{3,1,2,0:T(2,128)}, f32[20,2,50,80]{3,1,2,0:T(2,128)}, u32[]{:S(2)}, u32[]{:S(2)}) collective-permute-start(f32[20,2,50,80]{3,1,2,0:T(2,128)} %get-tuple-element.25), channel_id=1, source_target_pairs={{0,16},{4,20},{8,24},{12,28},{16,0},{20,4},{24,8},{28,12},{1,17},{... | collective-permute-start | bytes 1920008 | tf_op jit(solution)/shard_map/ppermute | solution.py:17
  216.4 90.2 %collective-permute-start.4 = (f32[20,2,50,80]{3,1,2,0:T(2,128)}, f32[20,2,50,80]{3,1,2,0:T(2,128)}, u32[]{:S(2)}, u32[]{:S(2)}) collective-permute-start(f32[20,2,50,80]{3,1,2,0:T(2,128)} %get-tuple-element.24), channel_id=1, source_target_pairs={{0,12},{4,16},{8,20},{12,24},{16,28},{20,0},{24,4},{28,8},{1,13},{... | collective-permute-start | bytes 1920008 | tf_op jit(solution)/shard_map/ppermute | solution.py:17
  237.3 70.7 %collective-permute-start.5 = (f32[20,2,50,80]{3,1,2,0:T(2,128)}, f32[20,2,50,80]{3,1,2,0:T(2,128)S(1)}, u32[]{:S(2)}, u32[]{:S(2)}) collective-permute-start(f32[20,2,50,80]{3,1,2,0:T(2,128)} %get-tuple-element.23), channel_id=1, source_target_pairs={{0,8},{4,12},{8,16},{12,20},{16,24},{20,28},{24,0},{28,4},{1,9},{5... | collective-permute-start | bytes 1920008 | tf_op jit(solution)/shard_map/ppermute | solution.py:17
  259.3 48.9 %collective-permute-start.6 = (f32[20,2,50,80]{3,1,2,0:T(2,128)}, f32[20,2,50,80]{3,1,2,0:T(2,128)S(1)}, u32[]{:S(2)}, u32[]{:S(2)}) collective-permute-start(f32[20,2,50,80]{3,1,2,0:T(2,128)} %get-tuple-element.22), channel_id=1, source_target_pairs={{0,4},{4,8},{8,12},{12,16},{16,20},{20,24},{24,28},{28,0},{1,5},{5... | collective-permute-start | bytes 1920008 | tf_op jit(solution)/shard_map/ppermute | solution.py:17
  318.0 24.0 %copy-start = (s32[640]{0:T(1024)S(1)}, s32[640]{0:T(1024)}, u32[]{:S(2)}) copy-start(s32[640]{0:T(1024)} %param.12) | copy-start | bytes 7684
  336.0 183.0 %all-to-all-start = ((f32[160,2,50,80]{0,1,2,3:T(2,128)}), f32[160,2,50,80]{0,1,2,3:T(2,128)}, u32[]{:S(2)}, u32[]{:S(2)}) async-start(f32[160,2,50,80]{0,1,2,3:T(2,128)} %copy.49), calls=%async_computation | async-start | bytes 16384000 | tf_op jit(solution)/shard_map/all_to_all | solution.py:62
